TPU v7x, 32 devices: a whole 2x2x4 slice. The times are simulated.
32 devices in a mesh: grp: 4 (over y, x), row: 8 (over z, core).
Axes of the slice: x: 2, y: 2, z: 4, core: 2. Of those that a mesh axis runs over, the one named last changes fastest.
Arguments:
- serving: bfloat16 [16384, 128], P('row'), may hold values from -1 to 1
- serving_scale: bfloat16 [128], P('row'), may hold values from 0.099609375 to 1
- hot_blocks: int32 [4, 16], P('grp', 'row'), may hold values from 0 to 15, as said below
- bag_lengths: int32 [32, 256], P(('grp', 'row')), may hold values from 1 to 16, 1024 in all within a row
- bag_indices: int32 [32, 1024], P(('grp', 'row')), may hold values from 0 to 2047, as said below
- dense_act: bfloat16 [8192, 128], P(('grp', 'row')), may hold values from -6 to 6
- labels: float32 [8192], P(('grp', 'row')), may hold values from 0 to 1
- w_top: bfloat16 [256, 1024], replicated, may hold values from -0.375 to 0.375
- w_out: float32 [1024], replicated, may hold values from -0.012 to 0.012
- master: float32 [4, 4096, 128], P('grp', 'row'), may hold values from -0.3 to 0.3
- accum: float32 [4, 4096], P('grp', 'row'), may hold values from 1e-05 to 0.0001
Outputs:
- new_master: float32 [4, 4096, 128], P('grp', 'row')
- new_accum: float32 [4, 4096], P('grp', 'row')
- new_serving: bfloat16 [16384, 128], P('row')
- new_scale: bfloat16 [128], P('row')
- top_grad: float32 [256, 1024], replicated
Inputs may be any that keep to these rules, and one draw needn't show every extreme that they name: `hot_blocks`: the 2 entries that one group names in one row shard are distinct. `bag_indices`: in each device's line, exactly 64 distinct values lie in each range of 256 consecutive positions that starts at a multiple of 256.
All inputs are finite; a program needn't handle non-finite values. Where the computation divides by a largest or mean magnitude, that divisor is 1e-20 or more.
Results may differ from a plain program's by a relative error of at most 0.012.
Values may be sent and summed in bfloat16 or wider, within the bound.
A program may use at most 128 MiB of HBM per device.

v0:
```python
import math
import jax
import jax.numpy as jnp
from jax import lax
from jax.sharding import PartitionSpec as P

BLOCK = 128
MOST = 16
lr_step = 0.05


def pool_grad(table, lengths, indices, dense_d, labels_d, w_top, w_out):
    rows, width = table.shape
    total = indices.shape[0]
    ends = jnp.cumsum(lengths)
    starts = ends - lengths
    slots = jnp.arange(MOST, dtype=jnp.int32)
    positions = jnp.minimum(starts[:, None] + slots[None, :], total - 1)
    picked = jnp.where(slots[None, :] < lengths[:, None], indices[positions], -1)
    span = math.gcd(rows, 2048)
    pieces = rows // span

    def count_block(first):
        columns = first + jnp.arange(span, dtype=jnp.int32)
        return jnp.sum((picked[:, :, None] == columns[None, None, :]).astype(jnp.bfloat16), axis=1)

    counts = lax.map(count_block, jnp.arange(pieces, dtype=jnp.int32) * span)
    table_blocks = table.reshape(pieces, span, width)

    def add_block(running, pair):
        block_counts, block_rows = pair
        return (
            running
            + jnp.dot(
                block_counts.astype(jnp.float32), block_rows, precision=lax.Precision.HIGHEST
            ),
            None,
        )

    pooled, _ = lax.scan(
        add_block, jnp.zeros((lengths.shape[0], width), jnp.float32), (counts, table_blocks)
    )
    joined = jnp.concatenate([pooled.astype(jnp.bfloat16), dense_d], axis=1)
    pre = jnp.dot(joined, w_top, preferred_element_type=jnp.float32)
    sig = jax.nn.sigmoid(pre)
    logit = jnp.dot(pre * sig, w_out, precision=lax.Precision.HIGHEST)
    dlogit = jax.nn.sigmoid(logit) - labels_d
    dpre = (dlogit[:, None] * w_out[None, :] * (sig * (1.0 + pre * (1.0 - sig)))).astype(
        jnp.bfloat16
    )
    top = lax.dot_general(
        joined, dpre, (((0,), (0,)), ((), ())), preferred_element_type=jnp.float32
    )
    dz = lax.dot_general(dpre, w_top, (((1,), (1,)), ((), ())), preferred_element_type=jnp.float32)
    emb_grad = dz[:, :width]

    def spread_block(block_counts):
        weights = block_counts.astype(jnp.float32)
        summed = lax.dot_general(
            weights, emb_grad, (((0,), (0,)), ((), ())), precision=lax.Precision.HIGHEST
        )
        return (summed, jnp.sum(weights, axis=0))

    hot, column_use = lax.map(spread_block, counts)
    return (top, hot.reshape(rows, width), column_use.reshape(rows) > 0)


def on_device(
    serving,
    serving_scale,
    hot_blocks,
    bag_lengths,
    bag_indices,
    dense_act,
    labels,
    w_top,
    w_out,
    master,
    accum,
):
    width = serving.shape[1]
    chosen = hot_blocks[0]
    count = chosen.shape[0]
    local_blocks = serving.reshape(-1, BLOCK, width)
    total_blocks = local_blocks.shape[0]
    picked = local_blocks[chosen]
    picked_scale = serving_scale[chosen]
    fetched, fetched_scale = (
        lax.all_gather(picked, "row", axis=0, tiled=True),
        lax.all_gather(picked_scale, "row", axis=0, tiled=True),
    )
    table = (
        fetched.astype(jnp.float32) * fetched_scale.astype(jnp.float32)[:, None, None]
    ).reshape(-1, width)
    top_part, hot_part, used_rows = pool_grad(
        table, bag_lengths[0], bag_indices[0], dense_act, labels, w_top, w_out
    )
    top_grad = lax.psum(top_part, ("grp", "row"))
    owned = lax.psum_scatter(hot_part, "row", scatter_dimension=0, tiled=True).reshape(
        count, BLOCK, width
    )
    quarter = lax.axis_index("grp")
    groups = lax.axis_size("grp")
    per_owner = total_blocks // groups
    arrived, arrived_ids = (
        lax.all_gather(owned, "grp", axis=0, tiled=True),
        lax.all_gather(chosen.astype(jnp.float32), "grp", axis=0, tiled=True),
    )
    slot = arrived_ids.astype(jnp.int32) - quarter * per_owner
    inside = (slot >= 0) & (slot < per_owner)
    slot = jnp.where(inside, slot, per_owner)
    grad = (
        jnp.zeros((per_owner, BLOCK, width), jnp.float32)
        .at[slot]
        .add(arrived, mode="drop")
        .reshape(-1, width)
    )
    weights = master[0]
    state = accum[0]
    new_state = state + jnp.mean(grad * grad, axis=1)
    new_weights = weights - lr_step * grad / jnp.sqrt(new_state)[:, None]
    scale_new = (
        jnp.max(jnp.abs(new_weights.reshape(per_owner, BLOCK * width)), axis=1) + 1e-06
    ).astype(jnp.bfloat16)
    coded = (
        (
            new_weights.reshape(per_owner, BLOCK, width)
            / scale_new.astype(jnp.float32)[:, None, None]
        )
        .astype(jnp.bfloat16)
        .reshape(-1, width)
    )
    fresh, fresh_scale = (
        lax.all_gather(coded, "grp", axis=0, tiled=True),
        lax.all_gather(scale_new, "grp", axis=0, tiled=True),
    )
    return (new_weights[None], new_state[None], fresh, fresh_scale, top_grad)


def solution(mesh):
    return jax.shard_map(
        on_device,
        mesh=mesh,
        in_specs=(
            P("row", None),
            P("row"),
            P("grp", "row"),
            P(("grp", "row"), None),
            P(("grp", "row"), None),
            P(("grp", "row"), None),
            P(("grp", "row")),
            P(),
            P(),
            P("grp", "row", None),
            P("grp", "row"),
        ),
        out_specs=(P("grp", "row", None), P("grp", "row"), P("row", None), P("row"), P()),
        check_vma=False,
    )
```

profile of v0, /device:TPU:0, one launch (start us, length us, event | category | flops | bytes accessed | tf_op | source)
XLA Modules:
  0.0 261.1 jit_solution(4268729098067179809)
XLA Ops:
  8.1 1.0 reduce-window.9
  9.3 0.8 bitcast_subtract_fusion
  10.4 16.7 %gather_fusion = s32[4096]{0:T(1024)S(1)} fusion(s32[1024]{0:T(1024)S(1)} %bitcast.46, s32[4096]{0:T(1024)S(1)} %broadcast_clamp_fusion), kind=kCustom, calls=%fused_computation | custom fusion | bytes 49152 | tf_op jit(solution)/shard_map/gather | solution.py:19
  27.3 0.6 dynamic-slice.2
  28.6 0.6 gather_fusion.2
  29.5 10.4 %fusion.1 = bf16[256,2048]{1,0:T(8,128)(2,1)S(1)} fusion(s32[256,16]{1,0:T(8,128)S(1)} %fusion.8), kind=kLoop, calls=%fused_computation.6 | loop fusion | flops 24641536 | bytes 1064960 | tf_op jit(solution)/shard_map/while/body/eval_jaxpr/reduce_sum | solution.py:25
  39.9 18.1 %all-reduce.1 = bf16[16]{0:T(256)(128)(2,1)S(1)} all-reduce(bf16[16]{0:T(256)(128)(2,1)S(1)} %dynamic-update-slice.1), channel_id=4, replica_groups=mesh['grp'=4,'row'=8] {'row'}, use_global_device_ids=true, to_apply=%add.1 | all-reduce | flops 16 | bytes 64
  58.0 0.6 gather_fusion.1
  58.6 15.1 %all-gather.1 = bf16[16,128,128]{2,1,0:T(8,128)(2,1)S(1)} all-gather(bf16[2,128,128]{2,1,0:T(8,128)(2,1)S(1)} %gather_fusion.1), channel_id=3, replica_groups=mesh['grp'=4,'row'=8] {'row'}, dimensions={0}, use_global_device_ids=true | all-gather | bytes 589824 | tf_op jit(solution)/shard_map/all_gather | solution.py:89
  74.0 1.0 convolution_convert_fusion
  75.0 0.3 fusion.10
  75.3 0.4 copy-done.9
  75.7 1.1 fusion.2
  76.8 0.4 multiply_convert_fusion
  77.2 0.3 fusion.5
  77.5 2.2 fusion.18
  79.8 0.6 copy-done.12
  80.3 0.6 dynamic-slice.1
  81.7 9.9 %all-reduce = f32[8]{0:T(128)S(1)} all-reduce(f32[8]{0:T(128)S(1)} %bitcast_dynamic-update-slice_fusion), channel_id=2, replica_groups=mesh['grp'=4,'row'=8] {'grp'}, use_global_device_ids=true, to_apply=%add | all-reduce | flops 8 | bytes 64
  92.2 1.3 fusion.9
  93.5 17.2 %reduce-scatter.2.cloned.1.call-done = f32[256,128]{1,0:T(8,128)} async-done(((f32[2048,128]{1,0:T(8,128)}), f32[256,128]{1,0:T(8,128)}) %reduce-scatter.2.cloned.1.call-update) | async-done | bytes 131088 | tf_op jit(solution)/shard_map/reduce_scatter | solution.py:99
  110.8 10.3 %all_gather.21 = f32[8,128,128]{2,1,0:T(8,128)S(1)} all-gather(f32[2,128,128]{2,1,0:T(8,128)} %bitcast.51), channel_id=1, replica_groups=mesh['grp'=4,'row'=8] {'grp'}, dimensions={0}, use_global_device_ids=true | all-gather | bytes 655360 | tf_op jit(solution)/shard_map/all_gather | solution.py:106
  121.1 1.0 scatter_fusion
  122.4 0.8 abs_reduce_fusion
  123.3 0.2 dynamic-update-slice.2
  123.6 9.6 %all-reduce.2 = bf16[16]{0:T(256)(128)(2,1)} all-reduce(bf16[16]{0:T(256)(128)(2,1)S(1)} %dynamic-update-slice.2), channel_id=1, replica_groups=mesh['grp'=4,'row'=8] {'grp'}, use_global_device_ids=true, to_apply=%add.2 | all-reduce | flops 16 | bytes 64
  133.4 9.7 %all_gather.22 = bf16[2048,128]{1,0:T(8,128)(2,1)S(1)} all-gather(bf16[512,128]{1,0:T(8,128)(2,1)S(1)} %bitcast.50), channel_id=1, replica_groups=mesh['grp'=4,'row'=8] {'grp'}, dimensions={0}, use_global_device_ids=true | all-gather | bytes 655360 | tf_op jit(solution)/shard_map/all_gather | solution.py:134
  143.1 0.6 add.103
  143.6 107.6 %all-reduce.5.cloned.1.call-done = f32[256,1024]{1,0:T(8,128)} async-done(((f32[256,1024]{1,0:T(8,128)}), f32[256,1024]{1,0:T(8,128)}) %all-reduce.5.cloned.1.call-update) | async-done | bytes 1048592 | tf_op jit(solution)/shard_map/psum | solution.py:98
  251.3 0.8 copy.26
  252.1 0.6 copy-done.5
  252.7 1.0 copy.27
  (56 shorter events, 1.9 us)
Async XLA Ops:
  8.0 50.0 %copy-start = (bf16[2048,128]{1,0:T(8,128)(2,1)S(1)}, bf16[2048,128]{1,0:T(8,128)(2,1)}, u32[]{:S(2)}) copy-start(bf16[2048,128]{1,0:T(8,128)(2,1)} %param.11) | copy-start | bytes 1572868
  8.0 2.3 copy-start.1
  8.0 102.7 %reduce-scatter.2.cloned.1.call-start = ((), (), s32[]{:S(2)}) async-start(), calls=%async_computation.1 | async-start | bytes 1179648 | tf_op jit(solution)/shard_map/reduce_scatter | solution.py:99
  10.3 16.8 %copy-start.8 = (s32[1,256]{1,0:T(1,128)S(1)}, s32[1,256]{1,0:T(1,128)}, u32[]{:S(2)}) copy-start(s32[1,256]{1,0:T(1,128)} %param.14) | copy-start | bytes 3076
  10.3 16.9 %copy-start.11 = (s32[1,2]{1,0:T(1,128)S(1)}, s32[1,2]{1,0:T(1,128)}, u32[]{:S(2)}) copy-start(s32[1,2]{1,0:T(1,128)} %param.13) | copy-start | bytes 28
  10.3 17.0 %copy-start.13 = (u32[32]{0:T(128)S(1)}, u32[32]{0:T(128)}, u32[]{:S(2)}) copy-start(u32[32]{0:T(128)} %constant.82) | copy-start | bytes 388
  10.4 18.2 %copy-start.2 = (bf16[16]{0:T(256)(128)(2,1)S(1)}, bf16[16]{0:T(256)(128)(2,1)}, u32[]{:S(2)}) copy-start(bf16[16]{0:T(256)(128)(2,1)} %param.12) | copy-start | bytes 100
  29.2 44.5 %copy-start.6 = (bf16[256,128]{1,0:T(8,128)(2,1)S(1)}, bf16[256,128]{1,0:T(8,128)(2,1)}, u32[]{:S(2)}) copy-start(bf16[256,128]{1,0:T(8,128)(2,1)} %param.16) | copy-start | bytes 196612
  73.9 1.0 copy-start.3
  75.0 0.7 copy-start.9
  75.7 1.1 copy-start.10
  79.7 0.7 copy-start.12
  79.7 171.5 %all-reduce.5.cloned.1.call-start = ((), (), s32[]{:S(2)}) async-start(), calls=%async_computation.2 | async-start | bytes 2097152 | tf_op jit(solution)/shard_map/psum | solution.py:98
  121.1 1.2 copy-start.7
  121.1 1.2 copy-start.4
  251.3 1.4 copy-start.5
Sparse Core Ops, SparseCore 0:
  79.8 30.8 reduce-scatter.1
Sparse Core Ops, SparseCore 1:
  123.7 127.5 all-reduce.4
where the time goes:
time: 262 us; the launch traced here: 261 us
  waiting for transfers between devices  125 us (48%)
  blocking collectives  72.7 us (28%)
  local copies, waits for them, and re-layouts  23.5 us (9%)
  between operations  17.8 us (7%)
  other arithmetic  16 us (6%)
  matrix products  6.17 us (2%)
    psum x1, waiting for transfers between devices, on_device(): top_grad = lax.psum(top_part, ('grp', 'row'))  108 us
    unnamed x3, blocking collectives  37.6 us
    reduce_scatter x1, waiting for transfers between devices, on_device(): lax.psum_scatter(hot_part, 'row', scatter_dimension=0, tiled=True)  17.2 us
    gather x2, local copies, waits for them, and re-layouts, pool_grad(): indices[positions]  16.8 us
    all_gather x1, blocking collectives, on_device(): lax.all_gather(picked, 'row', axis=0, tiled=True)  15.1 us
    reduce_sum x1, other arithmetic, count_block(): jnp.sum((picked[:, :, None] == columns[None, None, :]).astype(jnp.bfloat1...  10.4 us
    all_gather x1, blocking collectives, on_device(): lax.all_gather(owned, 'grp', axis=0, tiled=True)  10.3 us
    all_gather x1, blocking collectives, on_device(): lax.all_gather(coded, 'grp', axis=0, tiled=True)  9.65 us
  transfers between devices with their start and end apart: 2, of which 2 were waited for; matrix products, arithmetic and copies ran while one was open for 1% of the time, Pallas kernels for 0%

commit v1 on v0

--- a/solution.py
+++ b/solution.py
@@ -7,6 +7,11 @@
 BLOCK = 128
 MOST = 16
 lr_step = 0.05
+
+
+def summed_here(x, mesh_axis):
+    parts = lax.all_gather(x, mesh_axis)
+    return jnp.sum(parts, axis=0)
 
 
 def pool_grad(table, lengths, indices, dense_d, labels_d, w_top, w_out):
@@ -95,7 +100,7 @@
     top_part, hot_part, used_rows = pool_grad(
         table, bag_lengths[0], bag_indices[0], dense_act, labels, w_top, w_out
     )
-    top_grad = lax.psum(top_part, ("grp", "row"))
+    top_grad = summed_here(top_part, ("grp", "row"))
     owned = lax.psum_scatter(hot_part, "row", scatter_dimension=0, tiled=True).reshape(
         count, BLOCK, width
     )

time: 262 us -> 311 us (1.19)
  waiting for transfers between devices: 125 us -> 152 us
  other arithmetic: 16 us -> 29.5 us
  blocking collectives: 72.7 us -> 81.3 us
    all_gather x0 -> x1, waiting for transfers between devices: none -> 121 us  [summed_here(): parts = lax.all_gather(x, mesh_axis)]
    psum x1 -> x0, waiting for transfers between devices: 108 us -> none  [on_device(): top_grad = lax.psum(top_part, ('grp', 'row'))]
    reduce_scatter x1, waiting for transfers between devices: 17.2 us -> 31.6 us  [on_device(): lax.psum_scatter(hot_part, 'row', scatter_dimension=0, tiled=True)]
    reduce_sum x0 -> x1, other arithmetic: none -> 12.8 us  [summed_here(): return jnp.sum(parts, axis=0)]
    all_gather x1, blocking collectives: 10.3 us -> 16.5 us  [on_device(): lax.all_gather(owned, 'grp', axis=0, tiled=True)]
  transfers between devices with their start and end apart: 2 -> 2, of which waited for: 2 -> 2; matrix products, arithmetic and copies ran while one was open for 1% -> 2% of each run, Pallas kernels for 0% -> 0%
where the time goes in v1:
time: 311 us; the launch traced here: 310 us
  waiting for transfers between devices  152 us (49%)
  blocking collectives  81.3 us (26%)
  other arithmetic  29.5 us (9%)
  local copies, waits for them, and re-layouts  23 us (7%)
  between operations  17.7 us (6%)
  matrix products  6.34 us (2%)
    all_gather x1, waiting for transfers between devices, summed_here(): parts = lax.all_gather(x, mesh_axis)  121 us
    unnamed x3, blocking collectives  37.9 us
    reduce_scatter x1, waiting for transfers between devices, on_device(): lax.psum_scatter(hot_part, 'row', scatter_dimension=0, tiled=True)  31.6 us
    gather x2, local copies, waits for them, and re-layouts, pool_grad(): indices[positions]  16.8 us
    all_gather x1, blocking collectives, on_device(): lax.all_gather(owned, 'grp', axis=0, tiled=True)  16.5 us
    all_gather x1, blocking collectives, on_device(): lax.all_gather(picked, 'row', axis=0, tiled=True)  14.9 us
    reduce_sum x1, other arithmetic, summed_here(): return jnp.sum(parts, axis=0)  12.8 us
    all_gather x1, blocking collectives, on_device(): lax.all_gather(coded, 'grp', axis=0, tiled=True)  12 us
  transfers between devices with their start and end apart: 2, of which 2 were waited for; matrix products, arithmetic and copies ran while one was open for 2% of the time, Pallas kernels for 0%

profile of v1, /device:TPU:0, one launch (start us, length us, event | category | flops | bytes accessed | tf_op | source)
XLA Modules:
  0.0 310.1 jit_solution(13665816136296797830)
XLA Ops:
  8.1 0.7 fusion.12
  8.8 1.0 reduce-window.9
  9.9 1.2 dynamic-slice.2
  11.8 1.3 gather_fusion.2
  13.1 0.2 dynamic-update-slice.1
  13.4 18.1 %all-reduce.1 = bf16[16]{0:T(256)(128)(2,1)S(1)} all-reduce(bf16[16]{0:T(256)(128)(2,1)S(1)} %dynamic-update-slice.1), channel_id=4, replica_groups=mesh['grp'=4,'row'=8] {'row'}, use_global_device_ids=true, to_apply=%add.1 | all-reduce | flops 16 | bytes 64
  31.5 0.6 gather_fusion.1
  32.1 0.9 copy.19
  33.0 0.8 bitcast_subtract_fusion
  34.1 16.7 %gather_fusion = s32[4096]{0:T(1024)S(1)} fusion(s32[1024]{0:T(1024)S(1)} %bitcast.47, s32[4096]{0:T(1024)S(1)} %broadcast_clamp_fusion), kind=kCustom, calls=%fused_computation | custom fusion | bytes 49152 | tf_op jit(solution)/shard_map/gather | solution.py:24
  51.0 14.9 %all-gather.1 = bf16[16,128,128]{2,1,0:T(8,128)(2,1)S(1)} all-gather(bf16[2,128,128]{2,1,0:T(8,128)(2,1)S(1)} %gather_fusion.1), channel_id=3, replica_groups=mesh['grp'=4,'row'=8] {'row'}, dimensions={0}, use_global_device_ids=true | all-gather | bytes 589824 | tf_op jit(solution)/shard_map/all_gather | solution.py:94
  66.0 10.4 %fusion.1 = bf16[256,2048]{1,0:T(8,128)(2,1)S(1)} fusion(s32[256,16]{1,0:T(8,128)S(1)} %fusion.8), kind=kLoop, calls=%fused_computation.6 | loop fusion | flops 24641536 | bytes 1064960 | tf_op jit(solution)/shard_map/while/body/eval_jaxpr/reduce_sum | solution.py:30
  76.5 1.0 convolution_convert_fusion
  77.5 0.5 fusion.10
  78.0 1.1 fusion.2
  79.1 0.4 multiply_convert_fusion
  79.6 0.3 fusion.5
  79.9 2.2 fusion.18
  82.1 1.3 fusion.9
  83.4 0.6 dynamic-slice.1
  84.8 9.9 %all-reduce = f32[8]{0:T(128)S(1)} all-reduce(f32[8]{0:T(128)S(1)} %bitcast_dynamic-update-slice_fusion), channel_id=2, replica_groups=mesh['grp'=4,'row'=8] {'grp'}, use_global_device_ids=true, to_apply=%add | all-reduce | flops 8 | bytes 64
  95.4 31.6 %reduce-scatter.2.cloned.1.call-done = f32[256,128]{1,0:T(8,128)} async-done(((f32[2048,128]{1,0:T(8,128)}), f32[256,128]{1,0:T(8,128)}) %reduce-scatter.2.cloned.1.call-update) | async-done | bytes 131088 | tf_op jit(solution)/shard_map/reduce_scatter | solution.py:104
  126.9 16.5 %all_gather.27 = f32[8,128,128]{2,1,0:T(8,128)S(1)} all-gather(f32[2,128,128]{2,1,0:T(8,128)} %bitcast.53), channel_id=1, replica_groups=mesh['grp'=4,'row'=8] {'grp'}, dimensions={0}, use_global_device_ids=true | all-gather | bytes 655360 | tf_op jit(solution)/shard_map/all_gather | solution.py:111
  143.4 1.0 scatter_fusion
  144.7 0.8 abs_reduce_fusion
  145.6 0.2 dynamic-update-slice.2
  145.9 9.9 %all-reduce.2 = bf16[16]{0:T(256)(128)(2,1)} all-reduce(bf16[16]{0:T(256)(128)(2,1)S(1)} %dynamic-update-slice.2), channel_id=1, replica_groups=mesh['grp'=4,'row'=8] {'grp'}, use_global_device_ids=true, to_apply=%add.2 | all-reduce | flops 16 | bytes 64
  155.8 0.6 add.101
  156.5 12.0 %all_gather.28 = bf16[2048,128]{1,0:T(8,128)(2,1)S(1)} all-gather(bf16[512,128]{1,0:T(8,128)(2,1)S(1)} %bitcast.52), channel_id=1, replica_groups=mesh['grp'=4,'row'=8] {'grp'}, dimensions={0}, use_global_device_ids=true | all-gather | bytes 655360 | tf_op jit(solution)/shard_map/all_gather | solution.py:139
  168.5 120.6 %all-gather.6.cloned.1.call-done = f32[8192,1024]{1,0:T(8,128)} async-done(((f32[256,1024]{1,0:T(8,128)}), f32[8192,1024]{1,0:T(8,128)}) %all-gather.6.cloned.1.call-update) | async-done | bytes 33554448 | tf_op jit(solution)/shard_map/all_gather | solution.py:13
  289.1 12.8 %reduce_sum.33 = f32[256,1024]{1,0:T(8,128)} reduce(f32[32,256,1024]{2,1,0:T(8,128)} %bitcast.48, f32[]{:T(128)} %constant.20.clone.1), dimensions={0}, to_apply=%region_8.9 | reduce | flops 8126464 | bytes 34603012 | tf_op jit(solution)/shard_map/reduce_sum | solution.py:14
  301.9 0.8 copy.25
  (48 shorter events, 1.5 us)
Async XLA Ops:
  8.0 23.5 %copy-start = (bf16[2048,128]{1,0:T(8,128)(2,1)S(1)}, bf16[2048,128]{1,0:T(8,128)(2,1)}, u32[]{:S(2)}) copy-start(bf16[2048,128]{1,0:T(8,128)(2,1)} %param.11) | copy-start | bytes 1572868
  8.0 26.0 %copy-start.1 = (s32[1,1024]{1,0:T(1,128)S(1)}, s32[1,1024]{1,0:T(1,128)}, u32[]{:S(2)}) copy-start(s32[1,1024]{1,0:T(1,128)} %param.15) | copy-start | bytes 12292
  8.0 118.9 %reduce-scatter.2.cloned.1.call-start = ((), (), s32[]{:S(2)}) async-start(), calls=%async_computation.1 | async-start | bytes 1179648 | tf_op jit(solution)/shard_map/reduce_scatter | solution.py:104
  34.0 16.9 %copy-start.5 = (s32[1,256]{1,0:T(1,128)S(1)}, s32[1,256]{1,0:T(1,128)}, u32[]{:S(2)}) copy-start(s32[1,256]{1,0:T(1,128)} %param.14) | copy-start | bytes 3076
  34.0 43.5 %copy-start.2 = (bf16[256,1024]{1,0:T(8,128)(2,1)S(1)}, bf16[256,1024]{1,0:T(8,128)(2,1)}, u32[]{:S(2)}) copy-start(bf16[256,1024]{1,0:T(8,128)(2,1)} %param.18) | copy-start | bytes 1572868
  34.1 44.0 %copy-start.6 = (f32[1024]{0:T(1024)S(1)}, f32[1024]{0:T(1024)}, u32[]{:S(2)}) copy-start(f32[1024]{0:T(1024)} %param.19) | copy-start | bytes 12292
  34.1 45.1 %copy-start.7 = (f32[256]{0:T(256)S(1)}, f32[256]{0:T(256)}, u32[]{:S(2)}) copy-start(f32[256]{0:T(256)} %param.17) | copy-start | bytes 3076
  34.1 49.4 %copy-start.9 = (u32[32]{0:T(128)S(1)}, u32[32]{0:T(128)}, u32[]{:S(2)}) copy-start(u32[32]{0:T(128)} %constant.77) | copy-start | bytes 388
  34.1 50.6 %copy-start.8 = (s32[1,2]{1,0:T(1,128)S(1)}, s32[1,2]{1,0:T(1,128)}, u32[]{:S(2)}) copy-start(s32[1,2]{1,0:T(1,128)} %param.13) | copy-start | bytes 28
  34.1 110.5 %copy-start.4 = (f32[1,512]{1,0:T(1,128)S(1)}, f32[1,512]{1,0:T(1,128)}, u32[]{:S(2)}) copy-start(f32[1,512]{1,0:T(1,128)} %param.21) | copy-start | bytes 6148
  34.1 110.5 %copy-start.3 = (f32[1,512,128]{2,1,0:T(8,128)S(1)}, f32[1,512,128]{2,1,0:T(8,128)}, u32[]{:S(2)}) copy-start(f32[1,512,128]{2,1,0:T(8,128)} %param.20) | copy-start | bytes 786436
  82.1 207.0 %all-gather.6.cloned.1.call-start = ((), (), s32[]{:S(2)}) async-start(), calls=%async_computation.2 | async-start | bytes 34603008 | tf_op jit(solution)/shard_map/all_gather | solution.py:13
Sparse Core Ops, SparseCore 0:
  82.2 44.7 reduce-scatter.1
Sparse Core Ops, SparseCore 1:
  85.6 203.5 all-gather.5
